TPU v7x, 256 devices: a 8x8x2 block of a 8x8x16 slice. The times are simulated.
256 devices in a mesh: img: 2 (over z), ga: 16 (over y, core), band: 8 (over x).
Axes of the slice: x: 8, y: 8, z: 2, core: 2. Of those that a mesh axis runs over, the one named last changes fastest.
The devices are a block of a 8x8x16 slice.
Arguments:
- orbitals: bfloat16 [1536, 49152], P(('img', 'band'), 'ga'), parts along dimension 0, as said below
- kernel: float32 [49152], P('ga'), may hold values from 0.3 to 3
- block_vectors: bfloat16 [512, 49152], P(('img', 'band'), 'ga'), parts along dimension 0
Outputs:
- ace_vectors: bfloat16 [1536, 49152], P(('img', 'band'), 'ga'), parts along dimension 0
- exchange_block: bfloat16 [512, 49152], P(('img', 'band'), 'ga'), parts along dimension 0
There are 2 independent parts, one for each index of `img`. A program takes and returns all parts, laid end to end along the dimension named above; an argument that names none is the same for every part. Nothing has to cross between parts.
Inputs may be any that keep to these rules, and one draw needn't show every extreme that they name: `orbitals`: the bands of one image are linearly independent, and the block lies largely in their span.
All inputs are finite; a program needn't handle non-finite values.
Results may differ from a plain program's by a relative error of at most 0.02.
Values may be sent and summed in bfloat16 or wider, within the bound.
A program may use at most 64 MiB of HBM per device.

v0:
```python
import jax
import jax.numpy as jnp
from jax import lax
from jax.sharding import PartitionSpec as P


def over_pieces(shard, axis):
    pieces = lax.all_gather(shard, axis).astype(jnp.float32)
    return pieces.sum(axis=0)


def from_everyone(shard, axis):
    count = lax.axis_size(axis)
    return lax.all_to_all(
        jnp.broadcast_to(shard[None], (count, *shard.shape)), axis, 0, 0, tiled=True
    )


def in_order(pieces, dim):
    pieces = jnp.moveaxis(pieces, 0, dim)
    dims = pieces.shape
    return pieces.reshape(*dims[:dim], dims[dim] * dims[dim + 1], *dims[dim + 2 :])


def gathered_copies(shard, axis, dim):
    pieces = from_everyone(shard, axis)
    return in_order(pieces, dim)


def taken_together(shard, axis):
    return from_everyone(shard, axis).astype(jnp.float32).sum(axis=0)


def cut_along(shard, dim, count):
    dims = shard.shape
    pieces = shard.reshape(*dims[:dim], count, dims[dim] // count, *dims[dim + 1 :])
    return jnp.moveaxis(pieces, dim, 0)


def sent_and_summed(shard, axis, dim):
    pieces = cut_along(shard, dim, lax.axis_size(axis))
    arrived = lax.all_to_all(pieces, axis, split_axis=0, concat_axis=0, tiled=True)
    return arrived.astype(jnp.float32).sum(axis=0)


def contract_first(left, right):
    return lax.dot_general(left, right, (((0,), (0,)), ((), ())), precision=lax.Precision.HIGHEST)


def shards(orbitals, kernel, block_vectors):
    groups = lax.axis_size("ga")
    own_band = lax.axis_index("band")
    total_coeffs = orbitals.shape[1] * groups
    full_orbitals, full_block = (
        lax.all_gather(orbitals, "band", axis=0, tiled=True),
        lax.all_gather(block_vectors, "band", axis=0, tiled=True),
    )
    weighted = (-(full_orbitals.astype(jnp.float32) * kernel[None, :])).astype(jnp.bfloat16)
    own_rows = orbitals.shape[0]
    partial_rows = lax.dot_general(
        orbitals, weighted, (((1,), (1,)), ((), ())), preferred_element_type=jnp.float32
    )
    summed_rows = over_pieces(partial_rows.astype(jnp.bfloat16), "ga").astype(jnp.float32)
    margin = (
        -gathered_copies(summed_rows.astype(jnp.bfloat16), "band", 0).astype(summed_rows.dtype)
        / total_coeffs
    )
    factor = jnp.linalg.cholesky(margin)
    identity = jnp.eye(factor.shape[0], dtype=jnp.float32)
    inverse = lax.linalg.triangular_solve(factor, identity, left_side=True, lower=True)
    inverse_rows = lax.dynamic_slice_in_dim(inverse, own_band * own_rows, own_rows, 0)
    projector = jnp.dot(inverse_rows, weighted.astype(jnp.float32), precision=lax.Precision.HIGHEST)
    local_coupling = jnp.dot(
        projector, full_block.astype(jnp.float32).T, precision=lax.Precision.HIGHEST
    )
    coupling = (
        taken_together(local_coupling.astype(jnp.bfloat16), "ga").astype(jnp.float32) / total_coeffs
    )
    applied = sent_and_summed(
        (-contract_first(coupling, projector)).astype(jnp.bfloat16), "band", 0
    )
    return (projector.astype(jnp.bfloat16), applied.astype(jnp.bfloat16))


def solution(mesh):
    placed = (P(("img", "band"), "ga"), P("ga"), P(("img", "band"), "ga"))
    return jax.shard_map(
        shards,
        mesh=mesh,
        in_specs=placed,
        out_specs=(P(("img", "band"), "ga"), P(("img", "band"), "ga")),
        check_vma=False,
    )
```

profile of v0, /device:TPU:513, one launch (start us, length us, event | category | flops | bytes accessed | tf_op | source)
XLA Modules:
  0.0 510.3 jit_solution(14080767505893318742)
XLA Ops:
  8.0 80.9 %all-gather.5.cloned.1.call-done = bf16[768,3072]{1,0:T(8,128)(2,1)} async-done(((bf16[96,3072]{1,0:T(8,128)(2,1)}), bf16[768,3072]{1,0:T(8,128)(2,1)}) %all-gather.5.cloned.1.call-update) | async-done | bytes 4718608 | tf_op jit(solution)/shard_map/all_gather | solution.py:55
  89.0 4.8 fusion.21
  93.8 41.2 %all-gather.9.cloned.1.call-done = bf16[1536,768]{1,0:T(8,128)(2,1)} async-done(((bf16[96,768]{1,0:T(8,128)(2,1)}), bf16[1536,768]{1,0:T(8,128)(2,1)}) %all-gather.9.cloned.1.call-update) | async-done | bytes 2359312 | tf_op jit(solution)/shard_map/all_gather | solution.py:8
  134.9 2.0 reduce_sum.33
  136.9 1.1 broadcast_in_dim.5
  138.0 6.4 %all-to-all-start = ((bf16[8,96,768]{2,1,0:T(8,128)(2,1)}), bf16[8,96,768]{2,1,0:T(8,128)(2,1)S(1)}, u32[]{:S(2)}, u32[]{:S(2)}) async-start(bf16[8,96,768]{2,1,0:T(8,128)(2,1)} %broadcast_in_dim.5), calls=%async_computation | async-start | bytes 2359296 | tf_op jit(solution)/shard_map/all_to_all | solution.py:14
  146.3 1.6 fusion.25
  147.9 35.2 %all-to-all-done = bf16[8,96,768]{2,1,0:T(8,128)(2,1)S(1)} async-done(((bf16[8,96,768]{2,1,0:T(8,128)(2,1)}), bf16[8,96,768]{2,1,0:T(8,128)(2,1)S(1)}, u32[]{:S(2)}, u32[]{:S(2)}) %all-to-all-start) | async-done | bytes 1179680 | tf_op jit(solution)/shard_map/all_to_all | solution.py:14
  183.3 2.2 copy.7
  185.5 1.9 fusion.3
  187.4 1.5 copy-done.1
  188.9 11.7 %cholesky.165 = f32[128,128]{1,0:T(8,128)S(1)} custom-call(f32[128,128]{1,0:T(8,128)S(1)} %cholesky.424), custom_call_target="Cholesky" | custom-call | tf_op jit(solution)/shard_map/jit(cholesky)/cholesky | solution.py:68
  200.6 9.8 %custom-call.46 = f32[1,128,128]{1,2,0:T(8,128)S(1)} custom-call(f32[1,128,128]{2,1,0:T(8,128)S(1)} %get-tuple-element.45), custom_call_target="InvertDiagBlocksLowerTriangular" | custom-call | tf_op jit(solution)/shard_map/jit(cholesky)/cholesky | solution.py:68
  210.6 1.4 constant_dynamic-update-slice_fusion.15
  212.0 1.4 convolution_subtract_fusion.4
  213.4 11.7 %cholesky.188 = f32[128,128]{1,0:T(8,128)S(1)} custom-call(f32[128,128]{1,0:T(8,128)S(1)} %cholesky.428), custom_call_target="Cholesky" | custom-call | tf_op jit(solution)/shard_map/jit(cholesky)/cholesky | solution.py:68
  225.2 10.0 %custom-call.47 = f32[1,128,128]{1,2,0:T(8,128)S(1)} custom-call(f32[1,128,128]{2,1,0:T(8,128)S(1)} %get-tuple-element.42), custom_call_target="InvertDiagBlocksLowerTriangular" | custom-call | tf_op jit(solution)/shard_map/jit(cholesky)/cholesky | solution.py:68
  235.5 1.5 convolution_subtract_fusion.5
  237.1 11.7 %cholesky.354 = f32[128,128]{1,0:T(8,128)S(1)} custom-call(f32[128,128]{1,0:T(8,128)S(1)} %cholesky.433), custom_call_target="Cholesky" | custom-call | tf_op jit(solution)/shard_map/jit(cholesky)/cholesky | solution.py:68
  249.5 9.8 %custom-call.48 = f32[1,128,128]{1,2,0:T(8,128)S(1)} custom-call(f32[1,128,128]{2,1,0:T(8,128)S(1)} %get-tuple-element.39), custom_call_target="InvertDiagBlocksLowerTriangular" | custom-call | tf_op jit(solution)/shard_map/jit(cholesky)/cholesky | solution.py:68
  259.7 1.6 convolution_subtract_fusion.6
  261.2 12.2 %cholesky.373 = f32[128,128]{1,0:T(8,128)S(1)} custom-call(f32[128,128]{1,0:T(8,128)S(1)} %cholesky.438), custom_call_target="Cholesky" | custom-call | tf_op jit(solution)/shard_map/jit(cholesky)/cholesky | solution.py:68
  274.1 9.8 %custom-call.49 = f32[1,128,128]{1,2,0:T(8,128)S(1)} custom-call(f32[1,128,128]{2,1,0:T(8,128)S(1)} %get-tuple-element.36), custom_call_target="InvertDiagBlocksLowerTriangular" | custom-call | tf_op jit(solution)/shard_map/jit(cholesky)/cholesky | solution.py:68
  284.2 1.5 convolution_subtract_fusion.7
  285.7 11.7 %cholesky.392 = f32[128,128]{1,0:T(8,128)S(1)} custom-call(f32[128,128]{1,0:T(8,128)S(1)} %cholesky.443), custom_call_target="Cholesky" | custom-call | tf_op jit(solution)/shard_map/jit(cholesky)/cholesky | solution.py:68
  298.2 9.8 %custom-call.50 = f32[1,128,128]{1,2,0:T(8,128)S(1)} custom-call(f32[1,128,128]{2,1,0:T(8,128)S(1)} %get-tuple-element.33), custom_call_target="InvertDiagBlocksLowerTriangular" | custom-call | tf_op jit(solution)/shard_map/jit(cholesky)/cholesky | solution.py:68
  308.2 1.3 convolution_subtract_fusion.8
  309.5 11.9 %cholesky.410 = f32[128,128]{1,0:T(8,128)S(1)} custom-call(f32[128,128]{1,0:T(8,128)S(1)} %convolution_subtract_fusion.8), custom_call_target="Cholesky" | custom-call | tf_op jit(solution)/shard_map/jit(cholesky)/cholesky | solution.py:68
  326.5 1.6 select_select_fusion
  328.2 21.5 %while.1 = (s32[]{:T(128)}, f32[768,768]{1,0:T(8,128)}, s32[6,2]{0,1:T(2,128)S(1)}, f32[6,128,128]{2,1,0:T(8,128)}, s32[]{:T(128)}) while((s32[]{:T(128)}, f32[768,768]{1,0:T(8,128)}, s32[6,2]{0,1:T(2,128)S(1)}, f32[6,128,128]{2,1,0:T(8,128)}, s32[]{:T(128)}) %tuple.45), condition=%wide.while_cond, body=%wide.while_body.sunk | while | flops 2 | bytes 132705 | solution.py:70
  328.8 2.9 bitcast_dynamic-update-slice_fusion.2
  332.5 2.9 bitcast_dynamic-update-slice_fusion.2
  336.1 2.9 bitcast_dynamic-update-slice_fusion.2
  339.6 2.9 bitcast_dynamic-update-slice_fusion.2
  343.2 2.9 bitcast_dynamic-update-slice_fusion.2
  346.8 2.8 bitcast_dynamic-update-slice_fusion.2
  349.7 59.8 %custom-call.51 = f32[6,128,128]{1,2,0:T(8,128)S(1)} custom-call(f32[6,128,128]{2,1,0:T(8,128)} %get-tuple-element.9), custom_call_target="InvertDiagBlocksLowerTriangular" | custom-call | tf_op jit(solution)/shard_map/triangular_solve | solution.py:70
  409.4 1.2 constant_dynamic-update-slice_fusion.4
  410.6 1.5 convolution_subtract_fusion.2
  412.7 1.5 convolution_subtract_fusion.3
  414.7 2.0 convolution_subtract_fusion.1
  417.2 2.0 fusion.12
  419.8 2.3 convolution_subtract_fusion
  422.6 3.7 fusion.65
  426.4 3.0 convolution_convert_fusion
  429.4 27.4 %all_to_all.15 = bf16[16,96,256]{2,1,0:T(8,128)(2,1)S(1)} all-to-all(bf16[16,96,256]{2,1,0:T(8,128)(2,1)S(1)} %broadcast_in_dim.7), channel_id=1, replica_groups=mesh['img'=2,'ga'=16,'band'=8] {'ga'}, dimensions={0} | all-to-all | bytes 1572864 | tf_op jit(solution)/shard_map/all_to_all | solution.py:14
  456.9 2.7 fusion
  459.6 43.0 %all_to_all.16 = bf16[8,32,3072]{2,1,0:T(8,128)(2,1)S(1)} all-to-all(bf16[8,32,3072]{2,1,0:T(8,128)(2,1)S(1)} %bitcast.88), channel_id=1, replica_groups=mesh['img'=2,'ga'=16,'band'=8] {'band'}, dimensions={0} | all-to-all | bytes 3145728 | tf_op jit(solution)/shard_map/all_to_all | solution.py:42
  (63 shorter events, 15.6 us)
Async XLA Ops:
  7.2 81.8 %all-gather.5.cloned.1.call-start = ((), (), s32[]{:S(2)}) async-start(), calls=%async_computation.3 | async-start | bytes 5308416 | tf_op jit(solution)/shard_map/all_gather | solution.py:55
  8.0 127.0 %all-gather.9.cloned.1.call-start = ((), (), s32[]{:S(2)}) async-start(), calls=%async_computation.5 | async-start | bytes 2506752 | tf_op jit(solution)/shard_map/all_gather | solution.py:8
  138.0 45.0 %all-to-all-start = ((bf16[8,96,768]{2,1,0:T(8,128)(2,1)}), bf16[8,96,768]{2,1,0:T(8,128)(2,1)S(1)}, u32[]{:S(2)}, u32[]{:S(2)}) async-start(bf16[8,96,768]{2,1,0:T(8,128)(2,1)} %broadcast_in_dim.5), calls=%async_computation | async-start | bytes 2359296 | tf_op jit(solution)/shard_map/all_to_all | solution.py:14
  144.5 281.9 %all-gather.7.cloned.1.call-start = ((), (), s32[]{:S(2)}) async-start(), calls=%async_computation.4 | async-start | bytes 1769472 | tf_op jit(solution)/shard_map/all_gather | solution.py:56
  187.4 1.5 copy-start.1
  328.2 84.5 %copy-start = (f32[768,768]{1,0:T(8,128)S(1)}, f32[768,768]{1,0:T(8,128)}, u32[]{:S(2)}) copy-start(f32[768,768]{1,0:T(8,128)} %fusion.25) | copy-start | bytes 7077892
  414.7 7.9 %slice-start = ((s8[4718592]{0:T(1024)(128)(4,1)}), s8[4194304]{0:T(1024)(128)(4,1)S(1)}, s32[]{:S(2)}) async-start(s8[4718592]{0:T(1024)(128)(4,1)} %bitcast.90), calls=%async_computation.6 | async-start | bytes 8388608
  417.2 5.4 %slice-start.1 = ((s8[4718592]{0:T(1024)(128)(4,1)}), s8[524288]{0:T(1024)(128)(4,1)S(1)}, s32[]{:S(2)}) async-start(s8[4718592]{0:T(1024)(128)(4,1)} %bitcast.90), calls=%async_computation.7 | async-start | bytes 1048576
  419.2 3.4 copy-start.2
Sparse Core Ops, SparseCore 0:
  9.8 79.1 all-gather.4
  93.9 40.9 all-gather.8
  147.1 44.9 all-gather.6
where the time goes:
time: 514 us; the launch traced here: 510 us
  other arithmetic  193 us (38%)
  waiting for transfers between devices  159 us (31%)
  blocking collectives  70.4 us (14%)
  matrix products  37 us (7%)
  local copies, waits for them, and re-layouts  26.5 us (5%)
  between operations  18.2 us (4%)
  starting transfers between devices  6.6 us (1%)
    another operation x22, other arithmetic, shards(): factor = jnp.linalg.cholesky(margin)  124 us
    all_gather x1, waiting for transfers between devices, shards(): lax.all_gather(orbitals, 'band', axis=0, tiled=True)  80.9 us
    another operation x3, other arithmetic, shards(): lax.linalg.triangular_solve(factor, identity, left_side=True, lower=True)  61.4 us
    all_to_all x1, blocking collectives, sent_and_summed(): lax.all_to_all(pieces, axis, split_axis=0, concat_axis=0, tiled=True)  43 us
    all_gather x1, waiting for transfers between devices, over_pieces(): pieces = lax.all_gather(shard, axis).astype(jnp.float32)  41.2 us
    all_to_all x1, waiting for transfers between devices, from_everyone(): lax.all_to_all(jnp.broadcast_to(shard[None], (count, *shard.shape)), axis...  35.2 us
    all_to_all x1, blocking collectives, from_everyone(): lax.all_to_all(jnp.broadcast_to(shard[None], (count, *shard.shape)), axis...  27.4 us
    another operation x18, local copies, waits for them, and re-layouts  21.5 us
  transfers between devices with their start and end apart: 4, of which 3 were waited for; matrix products, arithmetic and copies ran while one was open for 47% of the time, Pallas kernels for 0%

commit v1 on v0

--- a/solution.py
+++ b/solution.py
@@ -1,7 +1,32 @@
+import functools
 import jax
 import jax.numpy as jnp
 from jax import lax
 from jax.sharding import PartitionSpec as P
+
+
+def _guide_cube(field, a_name):
+    formed, tmp, mixed_arr = (lax.psum(1, a_name), lax.axis_index(a_name), field.shape[0])
+    windows = [(p, (p + 1) % formed) for p in range(formed)]
+    store = [(p, (p - 1) % formed) for p in range(formed)]
+    value_now = jnp.zeros((*field.shape[:0], formed * mixed_arr, *field.shape[1:]), field.dtype)
+    value_now = lax.dynamic_update_slice_in_dim(value_now, field, tmp * mixed_arr, axis=0)
+    long_array = newest = field
+    wide_out = formed // 2
+    for s in range(1, wide_out + 1):
+        long_array = lax.ppermute(long_array, axis_name=a_name, perm=windows)
+        value_now = lax.dynamic_update_slice_in_dim(
+            value_now, long_array, (tmp - s) % formed * mixed_arr, axis=0
+        )
+        if s < formed - wide_out:
+            newest = lax.ppermute(newest, axis_name=a_name, perm=store)
+            value_now = lax.dynamic_update_slice_in_dim(
+                value_now, newest, (tmp + s) % formed * mixed_arr, axis=0
+            )
+    return value_now
+
+
+cut_pages = functools.partial(_guide_cube, a_name="band")
 
 
 def over_pieces(shard, axis):
@@ -52,7 +77,7 @@
     own_band = lax.axis_index("band")
     total_coeffs = orbitals.shape[1] * groups
     full_orbitals, full_block = (
-        lax.all_gather(orbitals, "band", axis=0, tiled=True),
+        cut_pages(orbitals),
         lax.all_gather(block_vectors, "band", axis=0, tiled=True),
     )
     weighted = (-(full_orbitals.astype(jnp.float32) * kernel[None, :])).astype(jnp.bfloat16)

time: 514 us -> 518 us (level)
  waiting for transfers between devices: 159 us -> 138 us
  starting transfers between devices: 6.6 us -> 23.9 us
    all_gather x1 -> x0, waiting for transfers between devices: 80.9 us -> none  [shards(): lax.all_gather(orbitals, 'band', axis=0, tiled=True)]
    ppermute x0 -> x7, waiting for transfers between devices: none -> 36.3 us  [the longest x4 36.3 us: _guide_cube(): long_array = lax.ppermute(long_array, axis_name=a_name, perm=windows)]
    all_gather x1, waiting for transfers between devices: 41.2 us -> 65.9 us  [over_pieces(): pieces = lax.all_gather(shard, axis).astype(jnp.float32)]
    ppermute x0 -> x7, starting transfers between devices: none -> 17.3 us  [the longest x4 9.39 us: _guide_cube(): long_array = lax.ppermute(long_array, axis_name=a_name, perm=windows)]
  transfers between devices with their start and end apart: 4 -> 10, of which waited for: 3 -> 6; matrix products, arithmetic and copies ran while one was open for 47% -> 47% of each run, Pallas kernels for 0% -> 0%
where the time goes in v1:
time: 518 us; the launch traced here: 510 us
  other arithmetic  193 us (37%)
  waiting for transfers between devices  138 us (27%)
  blocking collectives  70.3 us (14%)
  matrix products  34.5 us (7%)
  local copies, waits for them, and re-layouts  29.6 us (6%)
  starting transfers between devices  23.9 us (5%)
  between operations  20.2 us (4%)
    another operation x22, other arithmetic, shards(): factor = jnp.linalg.cholesky(margin)  124 us
    all_gather x1, waiting for transfers between devices, over_pieces(): pieces = lax.all_gather(shard, axis).astype(jnp.float32)  65.9 us
    another operation x3, other arithmetic, shards(): lax.linalg.triangular_solve(factor, identity, left_side=True, lower=True)  61.4 us
    all_to_all x1, blocking collectives, sent_and_summed(): lax.all_to_all(pieces, axis, split_axis=0, concat_axis=0, tiled=True)  42.9 us
    ppermute x4, waiting for transfers between devices, _guide_cube(): long_array = lax.ppermute(long_array, axis_name=a_name, perm=windows)  36.3 us
    all_to_all x1, waiting for transfers between devices, from_everyone(): lax.all_to_all(jnp.broadcast_to(shard[None], (count, *shard.shape)), axis...  35.6 us
    all_to_all x1, blocking collectives, from_everyone(): lax.all_to_all(jnp.broadcast_to(shard[None], (count, *shard.shape)), axis...  27.4 us
    another operation x18, local copies, waits for them, and re-layouts  21 us
  transfers between devices with their start and end apart: 10, of which 6 were waited for; matrix products, arithmetic and copies ran while one was open for 47% of the time, Pallas kernels for 0%

profile of v1, /device:TPU:513, one launch (start us, length us, event | category | flops | bytes accessed | tf_op | source)
XLA Modules:
  0.0 509.8 jit_solution(5847782982322109458)
XLA Ops:
  8.1 2.3 collective-permute-start
  10.4 2.3 collective-permute-start.1
  13.9 6.2 %collective-permute-done = bf16[96,3072]{1,0:T(8,128)(2,1)S(1)} collective-permute-done((bf16[96,3072]{1,0:T(8,128)(2,1)}, bf16[96,3072]{1,0:T(8,128)(2,1)S(1)}, u32[]{:S(2)}, u32[]{:S(2)}) %collective-permute-start) | collective-permute-done | bytes 589856 | tf_op jit(solution)/shard_map/ppermute | solution.py:17
  20.1 4.0 collective-permute-start.2
  24.1 2.9 collective-permute-start.3
  27.2 8.9 %collective-permute-done.2 = bf16[96,3072]{1,0:T(8,128)(2,1)S(1)} collective-permute-done((bf16[96,3072]{1,0:T(8,128)(2,1)S(1)}, bf16[96,3072]{1,0:T(8,128)(2,1)S(1)}, u32[]{:S(2)}, u32[]{:S(2)}) %collective-permute-start.2) | collective-permute-done | bytes 589856 | tf_op jit(solution)/shard_map/ppermute | solution.py:17
  36.0 2.7 collective-permute-start.5
  38.8 9.0 %collective-permute-done.4 = bf16[96,3072]{1,0:T(8,128)(2,1)S(1)} collective-permute-done((bf16[96,3072]{1,0:T(8,128)(2,1)S(1)}, bf16[96,3072]{1,0:T(8,128)(2,1)S(1)}, u32[]{:S(2)}, u32[]{:S(2)}) %collective-permute-start.4) | collective-permute-done | bytes 589856 | tf_op jit(solution)/shard_map/ppermute | solution.py:17
  47.8 3.1 collective-permute-start.6
  51.0 12.3 %collective-permute-done.6 = bf16[96,3072]{1,0:T(8,128)(2,1)S(1)} collective-permute-done((bf16[96,3072]{1,0:T(8,128)(2,1)S(1)}, bf16[96,3072]{1,0:T(8,128)(2,1)S(1)}, u32[]{:S(2)}, u32[]{:S(2)}) %collective-permute-start.6) | collective-permute-done | bytes 589856 | tf_op jit(solution)/shard_map/ppermute | solution.py:17
  63.4 2.1 copy-done.2
  65.5 2.3 fusion.21
  67.8 65.9 %all-gather.6.cloned.1.call-done = bf16[1536,768]{1,0:T(8,128)(2,1)} async-done(((bf16[96,768]{1,0:T(8,128)(2,1)}), bf16[1536,768]{1,0:T(8,128)(2,1)}) %all-gather.6.cloned.1.call-update) | async-done | bytes 2359312 | tf_op jit(solution)/shard_map/all_gather | solution.py:33
  133.7 2.0 reduce_sum.33
  136.8 6.4 %all-to-all-start = ((bf16[8,96,768]{2,1,0:T(8,128)(2,1)}), bf16[8,96,768]{2,1,0:T(8,128)(2,1)S(1)}, u32[]{:S(2)}, u32[]{:S(2)}) async-start(bf16[8,96,768]{2,1,0:T(8,128)(2,1)} %broadcast_in_dim.9), calls=%async_computation | async-start | bytes 2359296 | tf_op jit(solution)/shard_map/all_to_all | solution.py:39
  144.9 1.6 fusion.25
  146.5 35.6 %all-to-all-done = bf16[8,96,768]{2,1,0:T(8,128)(2,1)S(1)} async-done(((bf16[8,96,768]{2,1,0:T(8,128)(2,1)}), bf16[8,96,768]{2,1,0:T(8,128)(2,1)S(1)}, u32[]{:S(2)}, u32[]{:S(2)}) %all-to-all-start) | async-done | bytes 1179680 | tf_op jit(solution)/shard_map/all_to_all | solution.py:39
  182.3 2.2 copy.7
  184.5 1.9 fusion.3
  187.9 11.7 %cholesky.165 = f32[128,128]{1,0:T(8,128)S(1)} custom-call(f32[128,128]{1,0:T(8,128)S(1)} %cholesky.424), custom_call_target="Cholesky" | custom-call | tf_op jit(solution)/shard_map/jit(cholesky)/cholesky | solution.py:93
  199.8 9.8 %custom-call.46 = f32[1,128,128]{1,2,0:T(8,128)S(1)} custom-call(f32[1,128,128]{2,1,0:T(8,128)S(1)} %get-tuple-element.45), custom_call_target="InvertDiagBlocksLowerTriangular" | custom-call | tf_op jit(solution)/shard_map/jit(cholesky)/cholesky | solution.py:93
  212.5 11.7 %cholesky.188 = f32[128,128]{1,0:T(8,128)S(1)} custom-call(f32[128,128]{1,0:T(8,128)S(1)} %cholesky.428), custom_call_target="Cholesky" | custom-call | tf_op jit(solution)/shard_map/jit(cholesky)/cholesky | solution.py:93
  224.2 10.2 %custom-call.47 = f32[1,128,128]{1,2,0:T(8,128)S(1)} custom-call(f32[1,128,128]{2,1,0:T(8,128)S(1)} %get-tuple-element.42), custom_call_target="InvertDiagBlocksLowerTriangular" | custom-call | tf_op jit(solution)/shard_map/jit(cholesky)/cholesky | solution.py:93
  236.3 11.7 %cholesky.354 = f32[128,128]{1,0:T(8,128)S(1)} custom-call(f32[128,128]{1,0:T(8,128)S(1)} %cholesky.433), custom_call_target="Cholesky" | custom-call | tf_op jit(solution)/shard_map/jit(cholesky)/cholesky | solution.py:93
  248.7 9.8 %custom-call.48 = f32[1,128,128]{1,2,0:T(8,128)S(1)} custom-call(f32[1,128,128]{2,1,0:T(8,128)S(1)} %get-tuple-element.39), custom_call_target="InvertDiagBlocksLowerTriangular" | custom-call | tf_op jit(solution)/shard_map/jit(cholesky)/cholesky | solution.py:93
  258.9 1.6 convolution_subtract_fusion.6
  260.4 11.9 %cholesky.373 = f32[128,128]{1,0:T(8,128)S(1)} custom-call(f32[128,128]{1,0:T(8,128)S(1)} %cholesky.438), custom_call_target="Cholesky" | custom-call | tf_op jit(solution)/shard_map/jit(cholesky)/cholesky | solution.py:93
  273.1 9.8 %custom-call.49 = f32[1,128,128]{1,2,0:T(8,128)S(1)} custom-call(f32[1,128,128]{2,1,0:T(8,128)S(1)} %get-tuple-element.36), custom_call_target="InvertDiagBlocksLowerTriangular" | custom-call | tf_op jit(solution)/shard_map/jit(cholesky)/cholesky | solution.py:93
  284.6 11.7 %cholesky.392 = f32[128,128]{1,0:T(8,128)S(1)} custom-call(f32[128,128]{1,0:T(8,128)S(1)} %cholesky.443), custom_call_target="Cholesky" | custom-call | tf_op jit(solution)/shard_map/jit(cholesky)/cholesky | solution.py:93
  297.1 9.8 %custom-call.50 = f32[1,128,128]{1,2,0:T(8,128)S(1)} custom-call(f32[1,128,128]{2,1,0:T(8,128)S(1)} %get-tuple-element.33), custom_call_target="InvertDiagBlocksLowerTriangular" | custom-call | tf_op jit(solution)/shard_map/jit(cholesky)/cholesky | solution.py:93
  308.4 11.9 %cholesky.410 = f32[128,128]{1,0:T(8,128)S(1)} custom-call(f32[128,128]{1,0:T(8,128)S(1)} %convolution_subtract_fusion.8), custom_call_target="Cholesky" | custom-call | tf_op jit(solution)/shard_map/jit(cholesky)/cholesky | solution.py:93
  325.5 1.6 select_select_fusion
  327.1 21.0 %while.1 = (s32[]{:T(128)}, f32[768,768]{1,0:T(8,128)}, s32[6,2]{0,1:T(2,128)S(1)}, f32[6,128,128]{2,1,0:T(8,128)}, s32[]{:T(128)}) while((s32[]{:T(128)}, f32[768,768]{1,0:T(8,128)}, s32[6,2]{0,1:T(2,128)S(1)}, f32[6,128,128]{2,1,0:T(8,128)}, s32[]{:T(128)}) %tuple.45), condition=%wide.while_cond, body=%wide.while_body.sunk | while | flops 2 | bytes 132705 | solution.py:95
  327.8 3.0 bitcast_dynamic-update-slice_fusion.2
  331.3 2.9 bitcast_dynamic-update-slice_fusion.2
  334.9 2.9 bitcast_dynamic-update-slice_fusion.2
  338.3 2.9 bitcast_dynamic-update-slice_fusion.2
  341.8 2.9 bitcast_dynamic-update-slice_fusion.2
  345.3 2.8 bitcast_dynamic-update-slice_fusion.2
  348.1 59.8 %custom-call.51 = f32[6,128,128]{1,2,0:T(8,128)S(1)} custom-call(f32[6,128,128]{2,1,0:T(8,128)} %get-tuple-element.9), custom_call_target="InvertDiagBlocksLowerTriangular" | custom-call | tf_op jit(solution)/shard_map/triangular_solve | solution.py:95
  413.2 2.0 convolution_subtract_fusion.1
  415.7 2.0 fusion.12
  418.2 2.3 convolution_subtract_fusion
  421.1 3.7 fusion.65
  424.9 3.0 convolution_convert_fusion
  427.9 27.4 %all_to_all.15 = bf16[16,96,256]{2,1,0:T(8,128)(2,1)S(1)} all-to-all(bf16[16,96,256]{2,1,0:T(8,128)(2,1)S(1)} %broadcast_in_dim.10), channel_id=1, replica_groups=mesh['img'=2,'ga'=16,'band'=8] {'ga'}, dimensions={0} | all-to-all | bytes 1572864 | tf_op jit(solution)/shard_map/all_to_all | solution.py:39
  455.4 2.7 fusion
  458.1 42.9 %all_to_all.16 = bf16[8,32,3072]{2,1,0:T(8,128)(2,1)S(1)} all-to-all(bf16[8,32,3072]{2,1,0:T(8,128)(2,1)S(1)} %bitcast.88), channel_id=1, replica_groups=mesh['img'=2,'ga'=16,'band'=8] {'band'}, dimensions={0} | all-to-all | bytes 3145728 | tf_op jit(solution)/shard_map/all_to_all | solution.py:67
  (87 shorter events, 29.7 us)
Async XLA Ops:
  8.0 125.7 %all-gather.6.cloned.1.call-start = ((), (), s32[]{:S(2)}) async-start(), calls=%async_computation.4 | async-start | bytes 2506752 | tf_op jit(solution)/shard_map/all_gather | solution.py:33
  8.1 12.0 %collective-permute-start = (bf16[96,3072]{1,0:T(8,128)(2,1)}, bf16[96,3072]{1,0:T(8,128)(2,1)S(1)}, u32[]{:S(2)}, u32[]{:S(2)}) collective-permute-start(bf16[96,3072]{1,0:T(8,128)(2,1)} %param.3), channel_id=1, source_target_pairs={{0,1},{1,2},{2,3},{3,4},{4,5},{5,6},{6,7},{7,0},{8,9},{9,10},{10,1... | collective-permute-start | bytes 1769480 | tf_op jit(solution)/shard_map/ppermute | solution.py:17
  10.4 13.7 %collective-permute-start.1 = (bf16[96,3072]{1,0:T(8,128)(2,1)}, bf16[96,3072]{1,0:T(8,128)(2,1)S(1)}, u32[]{:S(2)}, u32[]{:S(2)}) collective-permute-start(bf16[96,3072]{1,0:T(8,128)(2,1)} %param.3), channel_id=1, source_target_pairs={{0,7},{1,0},{2,1},{3,2},{4,3},{5,4},{6,5},{7,6},{8,15},{9,8},{10,9... | collective-permute-start | bytes 1769480 | tf_op jit(solution)/shard_map/ppermute | solution.py:22
  12.7 1.1 copy-start.3
  20.1 16.0 %collective-permute-start.2 = (bf16[96,3072]{1,0:T(8,128)(2,1)S(1)}, bf16[96,3072]{1,0:T(8,128)(2,1)S(1)}, u32[]{:S(2)}, u32[]{:S(2)}) collective-permute-start(bf16[96,3072]{1,0:T(8,128)(2,1)S(1)} %collective-permute-done), channel_id=1, source_target_pairs={{0,1},{1,2},{2,3},{3,4},{4,5},{5,6},{6,7},{7,0},{8,9},{9,10},{10,1... | collective-permute-start | bytes 1769480 | tf_op jit(solution)/shard_map/ppermute | solution.py:17
  24.1 11.9 %collective-permute-start.3 = (bf16[96,3072]{1,0:T(8,128)(2,1)S(1)}, bf16[96,3072]{1,0:T(8,128)(2,1)S(1)}, u32[]{:S(2)}, u32[]{:S(2)}) collective-permute-start(bf16[96,3072]{1,0:T(8,128)(2,1)S(1)} %collective-permute-done.1), channel_id=1, source_target_pairs={{0,7},{1,0},{2,1},{3,2},{4,3},{5,4},{6,5},{7,6},{8,15},{9,8},{10,9... | collective-permute-start | bytes 1769480 | tf_op jit(solution)/shard_map/ppermute | solution.py:22
  36.0 11.8 %collective-permute-start.4 = (bf16[96,3072]{1,0:T(8,128)(2,1)S(1)}, bf16[96,3072]{1,0:T(8,128)(2,1)S(1)}, u32[]{:S(2)}, u32[]{:S(2)}) collective-permute-start(bf16[96,3072]{1,0:T(8,128)(2,1)S(1)} %collective-permute-done.2), channel_id=1, source_target_pairs={{0,1},{1,2},{2,3},{3,4},{4,5},{5,6},{6,7},{7,0},{8,9},{9,10},{10,1... | collective-permute-start | bytes 1769480 | tf_op jit(solution)/shard_map/ppermute | solution.py:17
  36.0 14.9 %collective-permute-start.5 = (bf16[96,3072]{1,0:T(8,128)(2,1)S(1)}, bf16[96,3072]{1,0:T(8,128)(2,1)S(1)}, u32[]{:S(2)}, u32[]{:S(2)}) collective-permute-start(bf16[96,3072]{1,0:T(8,128)(2,1)S(1)} %collective-permute-done.3), channel_id=1, source_target_pairs={{0,7},{1,0},{2,1},{3,2},{4,3},{5,4},{6,5},{7,6},{8,15},{9,8},{10,9... | collective-permute-start | bytes 1769480 | tf_op jit(solution)/shard_map/ppermute | solution.py:22
  38.8 26.7 %copy-start.4 = (f32[3072]{0:T(1024)S(1)}, f32[3072]{0:T(1024)}, u32[]{:S(2)}) copy-start(f32[3072]{0:T(1024)} %param.4) | copy-start | bytes 36868
  47.8 15.5 %collective-permute-start.6 = (bf16[96,3072]{1,0:T(8,128)(2,1)S(1)}, bf16[96,3072]{1,0:T(8,128)(2,1)S(1)}, u32[]{:S(2)}, u32[]{:S(2)}) collective-permute-start(bf16[96,3072]{1,0:T(8,128)(2,1)S(1)} %collective-permute-done.4), channel_id=1, source_target_pairs={{0,1},{1,2},{2,3},{3,4},{4,5},{5,6},{6,7},{7,0},{8,9},{9,10},{10,1... | collective-permute-start | bytes 1769480 | tf_op jit(solution)/shard_map/ppermute | solution.py:17
  63.4 2.1 copy-start.2
  136.8 45.2 %all-to-all-start = ((bf16[8,96,768]{2,1,0:T(8,128)(2,1)}), bf16[8,96,768]{2,1,0:T(8,128)(2,1)S(1)}, u32[]{:S(2)}, u32[]{:S(2)}) async-start(bf16[8,96,768]{2,1,0:T(8,128)(2,1)} %broadcast_in_dim.9), calls=%async_computation | async-start | bytes 2359296 | tf_op jit(solution)/shard_map/all_to_all | solution.py:39
  143.2 281.6 %all-gather.4.cloned.1.call-start = ((), (), s32[]{:S(2)}) async-start(), calls=%async_computation.3 | async-start | bytes 1769472 | tf_op jit(solution)/shard_map/all_gather | solution.py:81
  186.5 1.5 copy-start.1
  327.1 84.0 %copy-start = (f32[768,768]{1,0:T(8,128)S(1)}, f32[768,768]{1,0:T(8,128)}, u32[]{:S(2)}) copy-start(f32[768,768]{1,0:T(8,128)} %fusion.25) | copy-start | bytes 7077892
  413.2 7.9 %slice-start = ((s8[4718592]{0:T(1024)(128)(4,1)}), s8[4194304]{0:T(1024)(128)(4,1)S(1)}, s32[]{:S(2)}) async-start(s8[4718592]{0:T(1024)(128)(4,1)} %bitcast.89), calls=%async_computation.5 | async-start | bytes 8388608
  415.7 5.4 %slice-start.1 = ((s8[4718592]{0:T(1024)(128)(4,1)}), s8[524288]{0:T(1024)(128)(4,1)S(1)}, s32[]{:S(2)}) async-start(s8[4718592]{0:T(1024)(128)(4,1)} %bitcast.89), calls=%async_computation.6 | async-start | bytes 1048576
Sparse Core Ops, SparseCore 0:
  67.9 65.7 all-gather.5
Sparse Core Ops, SparseCore 1:
  145.5 45.1 all-gather.3
